TPU v7x, 32 devices: a whole 2x2x4 slice. The times are simulated.
32 devices in a mesh: orb: 16 (over z, y, core), grid: 2 (over x).
Axes of the slice: x: 2, y: 2, z: 4, core: 2. Of those that a mesh axis runs over, the one named last changes fastest.
Arguments:
- orbitals: bfloat16 [32, 11520], P('orb', 'grid'), may hold values from -1.5 to 1.5
- occupation: bfloat16 [32], P('orb'), may hold values from 0.29882812 to 1
Outputs:
- potentials: float32 [32, 11520], P('orb', 'grid')
- projectors: float32 [32, 11520], P('orb', 'grid')
All inputs are finite; a program needn't handle non-finite values.
Results may differ from a plain program's by a relative error of at most 0.0025.
Values may be sent and summed in bfloat16 or wider, within the bound.
No kernel may reach another device: no remote copies, remote signals or barrier semaphores. Data moves between devices by JAX's collectives and lax.ppermute only.
A program may use at most 64 MiB of HBM per device.

v0:
```python
import math
import jax
import jax.numpy as jnp
from jax import lax
from jax.sharding import PartitionSpec as P

NX = 20
NY = 24
NZ = 24
NPTS = 11520


def hartley_table(length):
    index = jnp.arange(length, dtype=jnp.int32)
    product = index[:, None] * index[None, :] % length
    angle = 2.0 * math.pi / length * product.astype(jnp.float32)
    return (jnp.cos(angle) + jnp.sin(angle)).astype(jnp.bfloat16)


def signed_square(length):
    index = jnp.arange(length, dtype=jnp.int32)
    signed = jnp.where(index <= length // 2, index, index - length).astype(jnp.float32)
    return (2.0 * math.pi * signed / length) ** 2


def coulomb_kernel(size_x, size_y, size_z):
    total = (
        signed_square(size_x)[:, None, None]
        + signed_square(size_y)[None, :, None]
        + signed_square(size_z)[None, None, :]
    )
    safe = jnp.where(total > 0, total, 1.0)
    return jnp.where(total > 0, 1.0 / safe, 0.0) / (size_x * size_y * size_z)


def solve_pairs(density, table_x, table_y, table_z, kernel):
    section = jnp.einsum(
        "ax,pxyz->payz", table_x, density, preferred_element_type=jnp.float32
    ).astype(jnp.bfloat16)
    section = jnp.einsum(
        "by,pxyz->pxbz", table_y, section, preferred_element_type=jnp.float32
    ).astype(jnp.bfloat16)
    spectrum = jnp.einsum("cz,pxyz->pxyc", table_z, section, preferred_element_type=jnp.float32)
    section = (spectrum * kernel).astype(jnp.bfloat16)
    section = jnp.einsum(
        "cz,pxyz->pxyc", table_z, section, preferred_element_type=jnp.float32
    ).astype(jnp.bfloat16)
    section = jnp.einsum(
        "by,pxyz->pxbz", table_y, section, preferred_element_type=jnp.float32
    ).astype(jnp.bfloat16)
    return jnp.einsum("ax,pxyz->payz", table_x, section, preferred_element_type=jnp.float32)


def pair_folder(targets, running, pieces):
    table_x = hartley_table(NX)
    table_y = hartley_table(NY)
    table_z = hartley_table(NZ)
    kernel = coulomb_kernel(NX, NY, NZ)
    target_rows = targets.astype(jnp.float32)
    target_count = targets.shape[0]
    block, block_weight = pieces
    rows = block.shape[0]
    group = math.gcd(rows, 64)
    blocks = block.reshape(rows // group, group, NPTS)
    weights = block_weight.astype(jnp.float32).reshape(rows // group, group)

    def accumulate(totals, inputs):
        sources, source_weight = inputs
        source_rows = sources.astype(jnp.float32)
        density = (target_rows[:, None, :] * source_rows[None, :, :]).astype(jnp.bfloat16)
        density = density.reshape(target_count * group, NX, NY, NZ)
        potential = solve_pairs(density, table_x, table_y, table_z, kernel).reshape(
            target_count, group, NPTS
        )
        weighted = source_weight[None, :, None] * potential * source_rows[None, :, :]
        return (totals - jnp.sum(weighted, axis=1), None)

    result, unused = lax.scan(accumulate, running, (blocks, weights))
    return result


def on_device(orbitals, occupation):
    own_count = orbitals.shape[0]
    per_device = own_count // lax.axis_size("grid")
    empty = jnp.zeros((per_device, NPTS), jnp.float32)
    whole = lax.all_gather(orbitals, "grid", axis=1, tiled=True)
    targets = lax.dynamic_slice_in_dim(whole, lax.axis_index("grid") * per_device, per_device, 0)
    totals = pair_folder(
        targets,
        empty,
        (
            lax.all_gather(whole, "orb", axis=0, tiled=True),
            lax.all_gather(occupation, "orb", axis=0, tiled=True),
        ),
    )
    potentials = lax.all_to_all(totals, "grid", split_axis=1, concat_axis=0, tiled=True)
    source_points, potential_points = (
        lax.all_to_all(
            orbitals.astype(jnp.float32), "orb", split_axis=1, concat_axis=0, tiled=True
        ),
        lax.all_to_all(potentials, "orb", split_axis=1, concat_axis=0, tiled=True),
    )
    partial_gram = (
        lax.dot_general(
            source_points,
            potential_points,
            (((1,), (1,)), ((), ())),
            precision=lax.Precision.HIGHEST,
        )
        / NPTS
    )
    gram = lax.psum(partial_gram, ("orb", "grid"))
    factor = jnp.linalg.cholesky(-gram)
    identity = jnp.eye(gram.shape[0], dtype=jnp.float32)
    inverse = lax.linalg.triangular_solve(factor, identity, left_side=True, lower=True)
    projector_points = jnp.dot(inverse, potential_points, precision=lax.Precision.HIGHEST)
    projectors = lax.all_to_all(projector_points, "orb", split_axis=0, concat_axis=1, tiled=True)
    return (potentials, projectors)


def solution(mesh):
    placed = (P("orb", "grid"), P("orb"))
    return jax.shard_map(
        on_device,
        mesh=mesh,
        in_specs=placed,
        out_specs=(P("orb", "grid"), P("orb", "grid")),
        check_vma=False,
    )
```

profile of v0, /device:TPU:0, one launch (start us, length us, event | category | flops | bytes accessed | tf_op | source)
XLA Modules:
  0.0 226.1 jit_solution(919936937522886090)
XLA Ops:
  0.7 5.7 %all_gather.10 = bf16[2,11520]{1,0:T(2,128)(2,1)S(1)} all-gather(bf16[2,5760]{1,0:T(2,128)(2,1)} %param.2), channel_id=1, replica_groups=mesh['orb'=16,'grid'=2] {'grid'}, dimensions={1}, use_global_device_ids=true | all-gather | bytes 69120 | tf_op jit(solution)/shard_map/all_gather | solution.py:86
  6.3 24.3 %all-gather = bf16[16,2,11520]{2,1,0:T(2,128)(2,1)S(1)} all-gather(bf16[1,2,11520]{2,1,0:T(2,128)(2,1)S(1)} %bitcast.58), channel_id=1, replica_groups=mesh['orb'=16,'grid'=2] {'orb'}, dimensions={0}, use_global_device_ids=true | all-gather | bytes 783360 | tf_op jit(solution)/shard_map/all_gather | solution.py:92
  30.7 6.4 %reshape.167 = f32[32,20,24,24]{3,2,1,0:T(8,128)} reshape(bf16[16,2,11520]{2,1,0:T(2,128)(2,1)S(1)} %all-gather) | data formatting | bytes 2211840 | tf_op jit(solution)/shard_map/while/body/eval_jaxpr/convert_element_type | solution.py:69
  37.1 1.3 reshape.174
  38.8 3.9 %multiply_convert_fusion.1 = bf16[32,20,24,24]{3,2,1,0:T(8,128)(2,1)S(1)} fusion(f32[32,20,24,24]{3,2,1,0:T(8,128)} %reshape.167, f32[20,24,24]{2,1,0:T(8,128)S(1)} %reshape.166), kind=kLoop, calls=%fused_computation.1 | loop fusion | flops 737280 | bytes 2257920 | tf_op jit(solution)/shard_map/while/body/eval_jaxpr/convert_element_type | solution.py:70
  42.6 4.9 %convert_bitcast_fusion = bf16[32,20,24,24]{1,3,2,0:T(8,128)(2,1)} fusion(bf16[32,20,24,24]{3,2,1,0:T(8,128)(2,1)S(1)} %multiply_convert_fusion.1), kind=kOutput, calls=%fused_computation.4 | convolution fusion | flops 15118640 | bytes 1474560 | tf_op jit(solution)/shard_map/while/body/eval_jaxpr/ax,pxyz->payz/dot_general | solution.py:37
  47.5 8.5 %copy.24 = bf16[32,20,24,24]{2,3,1,0:T(8,128)(2,1)} copy(bf16[32,20,24,24]{1,3,2,0:T(8,128)(2,1)} %convert_bitcast_fusion) | data formatting | bytes 1474560 | tf_op jit(solution)/shard_map/while/body/eval_jaxpr/convert_element_type | solution.py:39
  56.0 5.2 %fusion.44 = bf16[32,20,24,24]{3,2,1,0:T(8,128)(2,1)} fusion(bf16[32,20,24,24]{2,3,1,0:T(8,128)(2,1)} %copy.24), kind=kOutput, calls=%fused_computation.53 | convolution fusion | flops 17701056 | bytes 1474560 | tf_op jit(solution)/shard_map/while/body/eval_jaxpr/by,pxyz->pxbz/dot_general | solution.py:40
  61.5 7.4 %fusion.2 = bf16[32,20,24,24]{3,2,1,0:T(8,128)(2,1)} fusion(f32[20,24,24]{2,1,0:T(8,128)S(1)} %fusion.19, bf16[32,20,24,24]{3,2,1,0:T(8,128)(2,1)} %fusion.44), kind=kOutput, calls=%fused_computation.5 | convolution fusion | flops 36139392 | bytes 1520640 | tf_op jit(solution)/shard_map/while/body/eval_jaxpr/cz,pxyz->pxyc/dot_general | solution.py:45
  68.9 5.4 %convert_bitcast_fusion.1 = bf16[32,20,24,24]{2,3,1,0:T(8,128)(2,1)} fusion(bf16[32,20,24,24]{3,2,1,0:T(8,128)(2,1)} %fusion.2), kind=kOutput, calls=%fused_computation.8 | convolution fusion | flops 18069696 | bytes 1474560 | tf_op jit(solution)/shard_map/while/body/eval_jaxpr/by,pxyz->pxbz/dot_general | solution.py:48
  74.3 10.1 %copy.27 = bf16[32,20,24,24]{0,1,3,2:T(8,128)(2,1)S(1)} copy(bf16[32,20,24,24]{2,3,1,0:T(8,128)(2,1)} %convert_bitcast_fusion.1) | data formatting | bytes 1474560 | tf_op jit(solution)/shard_map/while/body/eval_jaxpr/convert_element_type | solution.py:50
  84.4 4.0 %convolution_bitcast_fusion = f32[32,20,24,24]{0,1,3,2:T(8,128)} fusion(bf16[32,20,24,24]{0,1,3,2:T(8,128)(2,1)S(1)} %copy.27), kind=kOutput, calls=%fused_computation.13 | convolution fusion | flops 14750000 | bytes 2211840 | tf_op jit(solution)/shard_map/while/body/eval_jaxpr/ax,pxyz->payz/dot_general | solution.py:51
  88.4 12.1 %copy.28 = f32[32,20,24,24]{3,2,1,0:T(8,128)} copy(f32[32,20,24,24]{0,1,3,2:T(8,128)} %convolution_bitcast_fusion) | data formatting | bytes 2949120 | tf_op jit(solution)/shard_map/while/body/eval_jaxpr/ax,pxyz->payz/transpose | solution.py:51
  102.0 6.8 %reshape.165 = f32[32,11520]{1,0:T(8,128)S(1)} reshape(f32[32,20,24,24]{3,2,1,0:T(8,128)} %copy.28) | data formatting | bytes 2949120 | tf_op jit(solution)/shard_map/while/body/eval_jaxpr/reshape | solution.py:72
  108.9 29.9 %all-reduce = bf16[32]{0:T(256)(128)(2,1)S(1)} all-reduce(bf16[32]{0:T(256)(128)(2,1)S(1)} %dynamic-update-slice.3), channel_id=1, replica_groups=mesh['orb'=16,'grid'=2] {'orb'}, use_global_device_ids=true, to_apply=%add | all-reduce | flops 32 | bytes 128
  139.1 0.7 sub.25
  139.7 3.3 %all-to-all-start = ((f32[1,2,5760]{2,0,1:T(1,128)}), f32[1,2,5760]{2,0,1:T(1,128)S(1)}, u32[]{:S(2)}, u32[]{:S(2)}) async-start(f32[1,2,5760]{2,0,1:T(1,128)} %sub.25), calls=%async_computation | async-start | bytes 92160 | tf_op jit(solution)/shard_map/all_to_all | solution.py:96
  143.8 3.2 %all-to-all-done = f32[1,2,5760]{2,0,1:T(1,128)S(1)} async-done(((f32[1,2,5760]{2,0,1:T(1,128)}), f32[1,2,5760]{2,0,1:T(1,128)S(1)}, u32[]{:S(2)}, u32[]{:S(2)}) %all-to-all-start) | async-done | bytes 46112 | tf_op jit(solution)/shard_map/all_to_all | solution.py:96
  147.0 3.5 %all-to-all-start.2 = ((f32[2,16,360]{2,0,1:T(2,128)}), f32[2,16,360]{2,0,1:T(2,128)S(1)}, u32[]{:S(2)}, u32[]{:S(2)}) async-start(f32[2,16,360]{2,0,1:T(2,128)} %copy.30), calls=%async_computation.2 | async-start | bytes 98304 | tf_op jit(solution)/shard_map/all_to_all | solution.py:98
  150.8 0.6 copy.29
  151.4 5.8 %all-to-all-done.2 = f32[2,16,360]{2,0,1:T(2,128)S(1)} async-done(((f32[2,16,360]{2,0,1:T(2,128)}), f32[2,16,360]{2,0,1:T(2,128)S(1)}, u32[]{:S(2)}, u32[]{:S(2)}) %all-to-all-start.2) | async-done | bytes 46112 | tf_op jit(solution)/shard_map/all_to_all | solution.py:98
  157.3 3.5 %all-to-all-start.1 = ((f32[2,16,360]{2,0,1:T(2,128)}), f32[2,16,360]{2,0,1:T(2,128)S(1)}, u32[]{:S(2)}, u32[]{:S(2)}) async-start(f32[2,16,360]{2,0,1:T(2,128)} %copy.29), calls=%async_computation.1 | async-start | bytes 98304 | tf_op jit(solution)/shard_map/all_to_all | solution.py:101
  160.8 6.7 %all-to-all-done.1 = f32[2,16,360]{2,0,1:T(2,128)S(1)} async-done(((f32[2,16,360]{2,0,1:T(2,128)}), f32[2,16,360]{2,0,1:T(2,128)S(1)}, u32[]{:S(2)}, u32[]{:S(2)}) %all-to-all-start.1) | async-done | bytes 46112 | tf_op jit(solution)/shard_map/all_to_all | solution.py:101
  167.8 38.0 %psum.7 = f32[32,32]{0,1:T(8,128)S(1)} all-reduce(f32[32,32]{0,1:T(8,128)S(1)} %fusion.17), channel_id=1, replica_groups=mesh['orb'=16,'grid'=2] {'orb','grid'}, use_global_device_ids=true, to_apply=%region_1.2 | all-reduce | flops 1024 | bytes 8192 | tf_op jit(solution)/shard_map/psum | solution.py:112
  205.8 2.9 %cholesky.17 = f32[32,32]{1,0:T(8,128)S(1)} custom-call(f32[32,32]{1,0:T(8,128)S(1)} %fusion.22), custom_call_target="Cholesky" | custom-call | tf_op jit(solution)/shard_map/jit(cholesky)/cholesky | solution.py:113
  208.8 0.6 compare_reduce_fusion
  209.4 0.7 fusion.21
  210.1 2.4 %custom-call.6 = f32[1,32,32]{1,2,0:T(8,128)S(1)} custom-call(f32[1,32,32]{2,1,0:T(8,128)S(1)} %fusion.21), custom_call_target="InvertDiagBlocksLowerTriangular" | custom-call | tf_op jit(solution)/shard_map/triangular_solve | solution.py:115
  213.0 0.6 copy.34
  213.6 5.0 %all-to-all-start.3 = ((f32[16,2,360]{2,1,0:T(2,128)}), f32[16,2,360]{2,1,0:T(2,128)S(1)}, u32[]{:S(2)}, u32[]{:S(2)}) async-start(f32[16,2,360]{2,1,0:T(2,128)} %copy.34), calls=%async_computation.3 | async-start | bytes 98304 | tf_op jit(solution)/shard_map/all_to_all | solution.py:117
  219.3 6.1 %all-to-all-done.3 = f32[16,2,360]{2,1,0:T(2,128)S(1)} async-done(((f32[16,2,360]{2,1,0:T(2,128)}), f32[16,2,360]{2,1,0:T(2,128)S(1)}, u32[]{:S(2)}, u32[]{:S(2)}) %all-to-all-start.3) | async-done | bytes 46112 | tf_op jit(solution)/shard_map/all_to_all | solution.py:117
  225.4 0.8 all_to_all.65
  (37 shorter events, 4.2 us)
Async XLA Ops:
  88.4 12.1 %copy-start.3 = (u32[32]{0:T(128)S(1)}, u32[32]{0:T(128)}, u32[]{:S(2)}) copy-start(u32[32]{0:T(128)} %constant.125) | copy-start | bytes 388
  88.4 13.4 %copy-start.2 = (bf16[2]{0:T(256)(128)(2,1)S(1)}, bf16[2]{0:T(256)(128)(2,1)}, u32[]{:S(2)}) copy-start(bf16[2]{0:T(256)(128)(2,1)} %param.3) | copy-start | bytes 16
  102.0 36.7 %copy-start = (f32[32,11520]{1,0:T(8,128)S(1)}, f32[32,11520]{1,0:T(8,128)}, u32[]{:S(2)}) copy-start(f32[32,11520]{1,0:T(8,128)} %reshape.174) | copy-start | bytes 4423684
  102.0 41.0 %copy-start.1 = (bf16[2,5760]{1,0:T(2,128)(2,1)S(1)}, bf16[2,5760]{1,0:T(2,128)(2,1)}, u32[]{:S(2)}) copy-start(bf16[2,5760]{1,0:T(2,128)(2,1)} %param.2) | copy-start | bytes 69124
  139.7 7.3 %all-to-all-start = ((f32[1,2,5760]{2,0,1:T(1,128)}), f32[1,2,5760]{2,0,1:T(1,128)S(1)}, u32[]{:S(2)}, u32[]{:S(2)}) async-start(f32[1,2,5760]{2,0,1:T(1,128)} %sub.25), calls=%async_computation | async-start | bytes 92160 | tf_op jit(solution)/shard_map/all_to_all | solution.py:96
  147.0 10.2 %all-to-all-start.2 = ((f32[2,16,360]{2,0,1:T(2,128)}), f32[2,16,360]{2,0,1:T(2,128)S(1)}, u32[]{:S(2)}, u32[]{:S(2)}) async-start(f32[2,16,360]{2,0,1:T(2,128)} %copy.30), calls=%async_computation.2 | async-start | bytes 98304 | tf_op jit(solution)/shard_map/all_to_all | solution.py:98
  157.3 10.2 %all-to-all-start.1 = ((f32[2,16,360]{2,0,1:T(2,128)}), f32[2,16,360]{2,0,1:T(2,128)S(1)}, u32[]{:S(2)}, u32[]{:S(2)}) async-start(f32[2,16,360]{2,0,1:T(2,128)} %copy.29), calls=%async_computation.1 | async-start | bytes 98304 | tf_op jit(solution)/shard_map/all_to_all | solution.py:101
  213.6 11.8 %all-to-all-start.3 = ((f32[16,2,360]{2,1,0:T(2,128)}), f32[16,2,360]{2,1,0:T(2,128)S(1)}, u32[]{:S(2)}, u32[]{:S(2)}) async-start(f32[16,2,360]{2,1,0:T(2,128)} %copy.34), calls=%async_computation.3 | async-start | bytes 98304 | tf_op jit(solution)/shard_map/all_to_all | solution.py:117
where the time goes:
time: 227 us; the launch traced here: 226 us
  blocking collectives  97.9 us (43%)
  local copies, waits for them, and re-layouts  50.8 us (22%)
  matrix products  27.5 us (12%)
  waiting for transfers between devices  21.9 us (10%)
  starting transfers between devices  15.3 us (7%)
  other arithmetic  11.4 us (5%)
    psum x1, blocking collectives, on_device(): gram = lax.psum(partial_gram, ('orb', 'grid'))  38 us
    unnamed x1, blocking collectives  29.9 us
    all_gather x1, blocking collectives, on_device(): lax.all_gather(whole, 'orb', axis=0, tiled=True)  24.3 us
    transpose x1, local copies, waits for them, and re-layouts, solve_pairs(): jnp.einsum('ax,pxyz->payz', table_x, section, preferred_element_type=jnp....  12.1 us
    dot_general x2, matrix products, solve_pairs(): jnp.einsum('by,pxyz->pxbz', table_y, section, preferred_element_type=jnp....  10.6 us
    convert_element_type x1, local copies, waits for them, and re-layouts, solve_pairs(): section = jnp.einsum('by,pxyz->pxbz', table_y, section, preferred_element...  10.1 us
    convert_element_type x1, local copies, waits for them, and re-layouts, solve_pairs(): section = jnp.einsum('ax,pxyz->payz', table_x, density, preferred_element...  8.51 us
    convert_element_type x2, local copies, waits for them, and re-layouts, accumulate(): source_rows = sources.astype(jnp.float32)  7.76 us
  transfers between devices with their start and end apart: 4, of which 4 were waited for; matrix products, arithmetic and copies ran while one was open for 1% of the time, Pallas kernels for 0%

commit v1 on v0

--- a/solution.py
+++ b/solution.py
@@ -109,7 +109,9 @@
         )
         / NPTS
     )
-    gram = lax.psum(partial_gram, ("orb", "grid"))
+    gram = partial_gram
+    for mesh_axis in ("grid", "orb"):
+        gram = lax.psum(gram, mesh_axis)
     factor = jnp.linalg.cholesky(-gram)
     identity = jnp.eye(gram.shape[0], dtype=jnp.float32)
     inverse = lax.linalg.triangular_solve(factor, identity, left_side=True, lower=True)

time: 227 us -> 252 us (1.11)
  blocking collectives: 97.9 us -> 124 us
    psum x1 -> x2, blocking collectives: 38 us -> 64.3 us  [on_device(): gram = lax.psum(gram, mesh_axis)]
where the time goes in v1:
time: 252 us; the launch traced here: 251 us
  blocking collectives  124 us (49%)
  local copies, waits for them, and re-layouts  50.8 us (20%)
  matrix products  27.5 us (11%)
  waiting for transfers between devices  21.8 us (9%)
  starting transfers between devices  13.8 us (5%)
  other arithmetic  11.4 us (5%)
    psum x2, blocking collectives, on_device(): gram = lax.psum(gram, mesh_axis)  64.3 us
    unnamed x1, blocking collectives  29.9 us
    all_gather x1, blocking collectives, on_device(): lax.all_gather(whole, 'orb', axis=0, tiled=True)  24.3 us
    transpose x1, local copies, waits for them, and re-layouts, solve_pairs(): jnp.einsum('ax,pxyz->payz', table_x, section, preferred_element_type=jnp....  12.1 us
    dot_general x2, matrix products, solve_pairs(): jnp.einsum('by,pxyz->pxbz', table_y, section, preferred_element_type=jnp....  10.6 us
    convert_element_type x1, local copies, waits for them, and re-layouts, solve_pairs(): section = jnp.einsum('by,pxyz->pxbz', table_y, section, preferred_element...  10.1 us
    convert_element_type x1, local copies, waits for them, and re-layouts, solve_pairs(): section = jnp.einsum('ax,pxyz->payz', table_x, density, preferred_element...  8.51 us
    convert_element_type x2, local copies, waits for them, and re-layouts, accumulate(): source_rows = sources.astype(jnp.float32)  7.76 us
  transfers between devices with their start and end apart: 4, of which 4 were waited for; matrix products, arithmetic and copies ran while one was open for 1% of the time, Pallas kernels for 0%

profile of v1, /device:TPU:0, one launch (start us, length us, event | category | flops | bytes accessed | tf_op | source)
XLA Modules:
  0.0 250.9 jit_solution(6524610204877749692)
XLA Ops:
  0.7 5.7 %all_gather.10 = bf16[2,11520]{1,0:T(2,128)(2,1)S(1)} all-gather(bf16[2,5760]{1,0:T(2,128)(2,1)} %param.2), channel_id=1, replica_groups=mesh['orb'=16,'grid'=2] {'grid'}, dimensions={1}, use_global_device_ids=true | all-gather | bytes 69120 | tf_op jit(solution)/shard_map/all_gather | solution.py:86
  6.3 24.3 %all-gather = bf16[16,2,11520]{2,1,0:T(2,128)(2,1)S(1)} all-gather(bf16[1,2,11520]{2,1,0:T(2,128)(2,1)S(1)} %bitcast.58), channel_id=1, replica_groups=mesh['orb'=16,'grid'=2] {'orb'}, dimensions={0}, use_global_device_ids=true | all-gather | bytes 783360 | tf_op jit(solution)/shard_map/all_gather | solution.py:92
  30.7 6.4 %reshape.167 = f32[32,20,24,24]{3,2,1,0:T(8,128)} reshape(bf16[16,2,11520]{2,1,0:T(2,128)(2,1)S(1)} %all-gather) | data formatting | bytes 2211840 | tf_op jit(solution)/shard_map/while/body/eval_jaxpr/convert_element_type | solution.py:69
  37.1 1.3 reshape.174
  38.8 3.9 %multiply_convert_fusion.1 = bf16[32,20,24,24]{3,2,1,0:T(8,128)(2,1)S(1)} fusion(f32[32,20,24,24]{3,2,1,0:T(8,128)} %reshape.167, f32[20,24,24]{2,1,0:T(8,128)S(1)} %reshape.166), kind=kLoop, calls=%fused_computation.1 | loop fusion | flops 737280 | bytes 2257920 | tf_op jit(solution)/shard_map/while/body/eval_jaxpr/convert_element_type | solution.py:70
  42.6 4.9 %convert_bitcast_fusion = bf16[32,20,24,24]{1,3,2,0:T(8,128)(2,1)} fusion(bf16[32,20,24,24]{3,2,1,0:T(8,128)(2,1)S(1)} %multiply_convert_fusion.1), kind=kOutput, calls=%fused_computation.4 | convolution fusion | flops 15118640 | bytes 1474560 | tf_op jit(solution)/shard_map/while/body/eval_jaxpr/ax,pxyz->payz/dot_general | solution.py:37
  47.5 8.5 %copy.24 = bf16[32,20,24,24]{2,3,1,0:T(8,128)(2,1)} copy(bf16[32,20,24,24]{1,3,2,0:T(8,128)(2,1)} %convert_bitcast_fusion) | data formatting | bytes 1474560 | tf_op jit(solution)/shard_map/while/body/eval_jaxpr/convert_element_type | solution.py:39
  56.0 5.2 %fusion.44 = bf16[32,20,24,24]{3,2,1,0:T(8,128)(2,1)} fusion(bf16[32,20,24,24]{2,3,1,0:T(8,128)(2,1)} %copy.24), kind=kOutput, calls=%fused_computation.53 | convolution fusion | flops 17701056 | bytes 1474560 | tf_op jit(solution)/shard_map/while/body/eval_jaxpr/by,pxyz->pxbz/dot_general | solution.py:40
  61.5 7.4 %fusion.2 = bf16[32,20,24,24]{3,2,1,0:T(8,128)(2,1)} fusion(f32[20,24,24]{2,1,0:T(8,128)S(1)} %fusion.19, bf16[32,20,24,24]{3,2,1,0:T(8,128)(2,1)} %fusion.44), kind=kOutput, calls=%fused_computation.5 | convolution fusion | flops 36139392 | bytes 1520640 | tf_op jit(solution)/shard_map/while/body/eval_jaxpr/cz,pxyz->pxyc/dot_general | solution.py:45
  68.9 5.4 %convert_bitcast_fusion.1 = bf16[32,20,24,24]{2,3,1,0:T(8,128)(2,1)} fusion(bf16[32,20,24,24]{3,2,1,0:T(8,128)(2,1)} %fusion.2), kind=kOutput, calls=%fused_computation.8 | convolution fusion | flops 18069696 | bytes 1474560 | tf_op jit(solution)/shard_map/while/body/eval_jaxpr/by,pxyz->pxbz/dot_general | solution.py:48
  74.3 10.1 %copy.27 = bf16[32,20,24,24]{0,1,3,2:T(8,128)(2,1)S(1)} copy(bf16[32,20,24,24]{2,3,1,0:T(8,128)(2,1)} %convert_bitcast_fusion.1) | data formatting | bytes 1474560 | tf_op jit(solution)/shard_map/while/body/eval_jaxpr/convert_element_type | solution.py:50
  84.4 4.0 %convolution_bitcast_fusion = f32[32,20,24,24]{0,1,3,2:T(8,128)} fusion(bf16[32,20,24,24]{0,1,3,2:T(8,128)(2,1)S(1)} %copy.27), kind=kOutput, calls=%fused_computation.13 | convolution fusion | flops 14750000 | bytes 2211840 | tf_op jit(solution)/shard_map/while/body/eval_jaxpr/ax,pxyz->payz/dot_general | solution.py:51
  88.4 12.1 %copy.28 = f32[32,20,24,24]{3,2,1,0:T(8,128)} copy(f32[32,20,24,24]{0,1,3,2:T(8,128)} %convolution_bitcast_fusion) | data formatting | bytes 2949120 | tf_op jit(solution)/shard_map/while/body/eval_jaxpr/ax,pxyz->payz/transpose | solution.py:51
  102.0 6.8 %reshape.165 = f32[32,11520]{1,0:T(8,128)S(1)} reshape(f32[32,20,24,24]{3,2,1,0:T(8,128)} %copy.28) | data formatting | bytes 2949120 | tf_op jit(solution)/shard_map/while/body/eval_jaxpr/reshape | solution.py:72
  108.9 29.9 %all-reduce = bf16[32]{0:T(256)(128)(2,1)S(1)} all-reduce(bf16[32]{0:T(256)(128)(2,1)S(1)} %dynamic-update-slice.3), channel_id=1, replica_groups=mesh['orb'=16,'grid'=2] {'orb'}, use_global_device_ids=true, to_apply=%add | all-reduce | flops 32 | bytes 128
  139.1 0.7 sub.25
  139.7 3.3 %all-to-all-start = ((f32[1,2,5760]{2,0,1:T(1,128)}), f32[1,2,5760]{2,0,1:T(1,128)S(1)}, u32[]{:S(2)}, u32[]{:S(2)}) async-start(f32[1,2,5760]{2,0,1:T(1,128)} %sub.25), calls=%async_computation | async-start | bytes 92160 | tf_op jit(solution)/shard_map/all_to_all | solution.py:96
  143.8 3.2 %all-to-all-done = f32[1,2,5760]{2,0,1:T(1,128)S(1)} async-done(((f32[1,2,5760]{2,0,1:T(1,128)}), f32[1,2,5760]{2,0,1:T(1,128)S(1)}, u32[]{:S(2)}, u32[]{:S(2)}) %all-to-all-start) | async-done | bytes 46112 | tf_op jit(solution)/shard_map/all_to_all | solution.py:96
  147.0 3.5 %all-to-all-start.2 = ((f32[2,16,360]{2,0,1:T(2,128)}), f32[2,16,360]{2,0,1:T(2,128)S(1)}, u32[]{:S(2)}, u32[]{:S(2)}) async-start(f32[2,16,360]{2,0,1:T(2,128)} %copy.30), calls=%async_computation.2 | async-start | bytes 98304 | tf_op jit(solution)/shard_map/all_to_all | solution.py:98
  150.8 0.6 copy.29
  151.4 5.8 %all-to-all-done.2 = f32[2,16,360]{2,0,1:T(2,128)S(1)} async-done(((f32[2,16,360]{2,0,1:T(2,128)}), f32[2,16,360]{2,0,1:T(2,128)S(1)}, u32[]{:S(2)}, u32[]{:S(2)}) %all-to-all-start.2) | async-done | bytes 46112 | tf_op jit(solution)/shard_map/all_to_all | solution.py:98
  157.3 3.5 %all-to-all-start.1 = ((f32[2,16,360]{2,0,1:T(2,128)}), f32[2,16,360]{2,0,1:T(2,128)S(1)}, u32[]{:S(2)}, u32[]{:S(2)}) async-start(f32[2,16,360]{2,0,1:T(2,128)} %copy.29), calls=%async_computation.1 | async-start | bytes 98304 | tf_op jit(solution)/shard_map/all_to_all | solution.py:101
  160.8 6.7 %all-to-all-done.1 = f32[2,16,360]{2,0,1:T(2,128)S(1)} async-done(((f32[2,16,360]{2,0,1:T(2,128)}), f32[2,16,360]{2,0,1:T(2,128)S(1)}, u32[]{:S(2)}, u32[]{:S(2)}) %all-to-all-start.1) | async-done | bytes 46112 | tf_op jit(solution)/shard_map/all_to_all | solution.py:101
  167.8 6.7 %psum.14 = f32[32,32]{0,1:T(8,128)S(1)} all-reduce(f32[32,32]{0,1:T(8,128)S(1)} %fusion.17), channel_id=1, replica_groups=mesh['orb'=16,'grid'=2] {'grid'}, use_global_device_ids=true, to_apply=%region_1.2 | all-reduce | flops 1024 | bytes 8192 | tf_op jit(solution)/shard_map/psum | solution.py:114
  174.5 57.6 %psum.15 = f32[32,32]{0,1:T(8,128)S(1)} all-reduce(f32[32,32]{0,1:T(8,128)S(1)} %psum.14), channel_id=1, replica_groups=mesh['orb'=16,'grid'=2] {'orb'}, use_global_device_ids=true, to_apply=%region_2.3 | all-reduce | flops 1024 | bytes 8192 | tf_op jit(solution)/shard_map/psum | solution.py:114
  232.2 2.9 %cholesky.17 = f32[32,32]{1,0:T(8,128)S(1)} custom-call(f32[32,32]{1,0:T(8,128)S(1)} %fusion.22), custom_call_target="Cholesky" | custom-call | tf_op jit(solution)/shard_map/jit(cholesky)/cholesky | solution.py:115
  235.8 0.7 fusion.21
  236.4 2.4 custom-call.6
  239.3 0.6 copy.34
  239.9 3.5 %all-to-all-start.3 = ((f32[16,2,360]{2,1,0:T(2,128)}), f32[16,2,360]{2,1,0:T(2,128)S(1)}, u32[]{:S(2)}, u32[]{:S(2)}) async-start(f32[16,2,360]{2,1,0:T(2,128)} %copy.34), calls=%async_computation.3 | async-start | bytes 98304 | tf_op jit(solution)/shard_map/all_to_all | solution.py:119
  244.1 6.1 %all-to-all-done.3 = f32[16,2,360]{2,1,0:T(2,128)S(1)} async-done(((f32[16,2,360]{2,1,0:T(2,128)}), f32[16,2,360]{2,1,0:T(2,128)S(1)}, u32[]{:S(2)}, u32[]{:S(2)}) %all-to-all-start.3) | async-done | bytes 46112 | tf_op jit(solution)/shard_map/all_to_all | solution.py:119
  250.2 0.8 all_to_all.65
  (38 shorter events, 4.8 us)
Async XLA Ops:
  88.4 12.1 %copy-start.3 = (u32[32]{0:T(128)S(1)}, u32[32]{0:T(128)}, u32[]{:S(2)}) copy-start(u32[32]{0:T(128)} %constant.125) | copy-start | bytes 388
  88.4 13.4 %copy-start.2 = (bf16[2]{0:T(256)(128)(2,1)S(1)}, bf16[2]{0:T(256)(128)(2,1)}, u32[]{:S(2)}) copy-start(bf16[2]{0:T(256)(128)(2,1)} %param.3) | copy-start | bytes 16
  102.0 36.7 %copy-start = (f32[32,11520]{1,0:T(8,128)S(1)}, f32[32,11520]{1,0:T(8,128)}, u32[]{:S(2)}) copy-start(f32[32,11520]{1,0:T(8,128)} %reshape.174) | copy-start | bytes 4423684
  102.0 41.0 %copy-start.1 = (bf16[2,5760]{1,0:T(2,128)(2,1)S(1)}, bf16[2,5760]{1,0:T(2,128)(2,1)}, u32[]{:S(2)}) copy-start(bf16[2,5760]{1,0:T(2,128)(2,1)} %param.2) | copy-start | bytes 69124
  139.7 7.3 %all-to-all-start = ((f32[1,2,5760]{2,0,1:T(1,128)}), f32[1,2,5760]{2,0,1:T(1,128)S(1)}, u32[]{:S(2)}, u32[]{:S(2)}) async-start(f32[1,2,5760]{2,0,1:T(1,128)} %sub.25), calls=%async_computation | async-start | bytes 92160 | tf_op jit(solution)/shard_map/all_to_all | solution.py:96
  147.0 10.2 %all-to-all-start.2 = ((f32[2,16,360]{2,0,1:T(2,128)}), f32[2,16,360]{2,0,1:T(2,128)S(1)}, u32[]{:S(2)}, u32[]{:S(2)}) async-start(f32[2,16,360]{2,0,1:T(2,128)} %copy.30), calls=%async_computation.2 | async-start | bytes 98304 | tf_op jit(solution)/shard_map/all_to_all | solution.py:98
  157.3 10.2 %all-to-all-start.1 = ((f32[2,16,360]{2,0,1:T(2,128)}), f32[2,16,360]{2,0,1:T(2,128)S(1)}, u32[]{:S(2)}, u32[]{:S(2)}) async-start(f32[2,16,360]{2,0,1:T(2,128)} %copy.29), calls=%async_computation.1 | async-start | bytes 98304 | tf_op jit(solution)/shard_map/all_to_all | solution.py:101
  239.9 10.2 %all-to-all-start.3 = ((f32[16,2,360]{2,1,0:T(2,128)}), f32[16,2,360]{2,1,0:T(2,128)S(1)}, u32[]{:S(2)}, u32[]{:S(2)}) async-start(f32[16,2,360]{2,1,0:T(2,128)} %copy.34), calls=%async_computation.3 | async-start | bytes 98304 | tf_op jit(solution)/shard_map/all_to_all | solution.py:119
